TPU v7x, 32 devices: a 4x4x1 block of a 4x4x8 slice. The times are simulated.
32 devices in a mesh: dp: 1 (over z), tp: 32 (over y, x, core).
Axes of the slice: x: 4, y: 4, z: 1, core: 2. Of those that a mesh axis runs over, the one named last changes fastest.
The devices are a block of a 4x4x8 slice.
Arguments:
- x_norm: bfloat16 [256, 5120], P(('dp', 'tp'))
- w_gate: bfloat16 [5120, 13824], P(None, 'tp')
- w_up: bfloat16 [5120, 13824], P(None, 'tp')
- w_down: bfloat16 [13824, 5120], P('tp')
- u_gate: bfloat16 [256, 13824], P('dp', 'tp')
- u_up: bfloat16 [256, 13824], P('dp', 'tp')
- grad_out: bfloat16 [256, 5120], P(('dp', 'tp'))
Outputs:
- output 1: bfloat16 [256, 5120], P(('dp', 'tp'))
- output 2: float32 [5120, 13824], P('dp', 'tp')
- output 3: float32 [5120, 13824], P('dp', 'tp')
- output 4: float32 [13824, 5120], P(('dp', 'tp'))
All inputs are finite; a program needn't handle non-finite values.
Results may differ from a plain program's by a relative error of at most 0.0134744.
Values are sent between devices in bfloat16 or wider.
A program may use at most 768 MiB of HBM per device.

v0:
```python
import jax
import jax.numpy as jnp
from jax import lax
from jax.sharding import PartitionSpec as P


def solution(mesh):
    group_size = mesh.shape['tp']
    contract_rows = (((0,), (0,)), ((), ()))
    contract_cols = (((1,), (1,)), ((), ()))

    def local_backward(x_loc, wg_loc, wu_loc, wd_loc, ug_loc, uu_loc, dy_loc):
        tok_local, hidden = x_loc.shape
        x_full = lax.all_gather(x_loc, 'tp', axis=0, tiled=True)
        dy_full = lax.all_gather(dy_loc, 'tp', axis=0, tiled=True)
        gate_f = ug_loc.astype(jnp.float32)
        up_f = uu_loc.astype(jnp.float32)
        sigmoid_g = jax.nn.sigmoid(gate_f)
        silu_g = gate_f * sigmoid_g
        z_act = (silu_g * up_f).astype(jnp.bfloat16)
        grad_wd = lax.dot_general(z_act, dy_full, contract_rows, preferred_element_type=jnp.float32)
        grad_mid = lax.dot_general(dy_full, wd_loc, contract_cols, preferred_element_type=jnp.float32)
        d_gate = (grad_mid * up_f * sigmoid_g * (1.0 + gate_f * (1.0 - sigmoid_g))).astype(jnp.bfloat16)
        d_up = (grad_mid * silu_g).astype(jnp.bfloat16)
        partial = (lax.dot_general(d_gate, wg_loc, contract_cols, preferred_element_type=jnp.float32)
                   + lax.dot_general(d_up, wu_loc, contract_cols, preferred_element_type=jnp.float32)).astype(jnp.bfloat16)
        received = lax.all_to_all(partial, 'tp', 0, 0, tiled=True)
        grad_x = received.reshape(group_size, tok_local, hidden).astype(jnp.float32).sum(axis=0).astype(jnp.bfloat16)
        grad_wg = lax.dot_general(x_full, d_gate, contract_rows, preferred_element_type=jnp.float32)
        grad_wu = lax.dot_general(x_full, d_up, contract_rows, preferred_element_type=jnp.float32)
        return grad_x, grad_wg, grad_wu, grad_wd

    row_spec = P(('dp', 'tp'), None)
    col_spec = P(None, 'tp')
    part_cols = P('dp', 'tp')
    return jax.shard_map(local_backward, mesh=mesh,
                         in_specs=(row_spec, col_spec, col_spec, P('tp', None), part_cols, part_cols, row_spec),
                         out_specs=(row_spec, part_cols, part_cols, row_spec),
                         check_vma=False)
```

profile of v0, /device:TPU:96, one launch (start us, length us, event | category | flops | bytes accessed | tf_op | source)
XLA Modules:
  0.0 130.8 jit_solution(13952100689734794584)
XLA Ops:
  7.2 0.1 all-gather.3.cloned.1.call-start
  7.2 0.7 all-gather.3.cloned.1.call-update
  8.0 0.1 all-gather.5.cloned.1.call-start
  8.0 0.7 all-gather.5.cloned.1.call-update
  8.8 42.8 %all-gather.3.cloned.1.call-done = bf16[256,5120]{1,0:T(8,128)(2,1)} async-done(((bf16[8,5120]{1,0:T(8,128)(2,1)}), bf16[256,5120]{1,0:T(8,128)(2,1)}) %all-gather.3.cloned.1.call-update) | async-done | bytes 2621456 | tf_op jit(solution)/shard_map/all_gather | solution.py:15
  51.6 0.0 copy-start.1
  51.6 4.6 %fusion.4 = (bf16[256,432]{0,1:T(8,128)(2,1)S(1)}, f32[256,432]{0,1:T(8,128)S(1)}) fusion(bf16[256,432]{0,1:T(8,128)(2,1)} %param.12, bf16[256,432]{0,1:T(8,128)(2,1)} %param.11, bf16[256,5120]{1,0:T(8,128)(2,1)} %all-gather.3.cloned.1.call-done, bf16[432,5120]{1,0:T(8,128)(2,1)} %param.10), kind=kOutput, calls=%fused_computation.12 | convolution fusion | flops 1133789184 | bytes 8151040 | tf_op jit(solution)/shard_map/dot_general | solution.py:22
  56.2 0.0 copy-done.1
  56.2 0.0 copy-start.2
  56.2 0.0 copy-start.4
  56.3 1.6 %fusion.13 = f32[256,5120]{1,0:T(8,128)S(1)} fusion(bf16[256,432]{0,1:T(8,128)(2,1)S(1)} %get-tuple-element.4, bf16[5120,432]{0,1:T(8,128)(2,1)S(1)} %copy-done.1), kind=kOutput, calls=%fused_computation.21 | convolution fusion | flops 1132462080 | bytes 9887744 | tf_op jit(solution)/shard_map/dot_general | solution.py:25
  57.9 0.6 copy-done.2
  58.5 0.0 copy-done.4
  58.5 3.2 %fusion.1 = bf16[32,8,5120]{2,1,0:T(8,128)(2,1)} fusion(f32[256,5120]{1,0:T(8,128)S(1)} %fusion.13, bf16[5120,432]{0,1:T(8,128)(2,1)S(1)} %copy-done.2, f32[256,432]{0,1:T(8,128)S(1)} %get-tuple-element.5, bf16[256,432]{0,1:T(8,128)(2,1)S(1)} %copy-done.4), kind=kOutput, calls=%fused_computation.4 | convolution fusion | flops 1135857664 | bytes 12951552 | tf_op jit(solution)/shard_map/dot_general | solution.py:26
  61.7 4.7 %all-to-all-start = ((bf16[32,8,5120]{2,1,0:T(8,128)(2,1)}), bf16[32,8,5120]{2,1,0:T(8,128)(2,1)S(1)}, u32[]{:S(2)}, u32[]{:S(2)}) async-start(bf16[32,8,5120]{2,1,0:T(8,128)(2,1)} %fusion.1), calls=%async_computation | async-start | bytes 5242880 | tf_op jit(solution)/shard_map/all_to_all | solution.py:27
  66.4 39.9 %all-gather.5.cloned.1.call-done = bf16[256,5120]{1,0:T(8,128)(2,1)} async-done(((bf16[8,5120]{1,0:T(8,128)(2,1)}), bf16[256,5120]{1,0:T(8,128)(2,1)}) %all-gather.5.cloned.1.call-update) | async-done | bytes 2621456 | tf_op jit(solution)/shard_map/all_gather | solution.py:14
  106.4 6.8 %convolution_bitcast_fusion.1 = f32[5120,432]{0,1:T(8,128)} fusion(bf16[256,432]{0,1:T(8,128)(2,1)S(1)} %get-tuple-element.4, bf16[256,5120]{1,0:T(8,128)(2,1)} %all-gather.5.cloned.1.call-done), kind=kOutput, calls=%fused_computation.1 | convolution fusion | flops 1132462080 | bytes 11689984 | tf_op jit(solution)/shard_map/dot_general | solution.py:29
  113.1 0.0 copy-done.3
  113.1 0.0 copy-done.5
  113.1 4.9 %fusion.10 = f32[432,5120]{1,0:T(8,128)} fusion(bf16[256,5120]{1,0:T(8,128)(2,1)S(1)} %copy-done.3, bf16[256,432]{0,1:T(8,128)(2,1)S(1)} %copy-done.5, bf16[256,432]{0,1:T(8,128)(2,1)S(1)} %copy-done.4), kind=kOutput, calls=%fused_computation.19 | convolution fusion | flops 1133346816 | bytes 11911168 | tf_op jit(solution)/shard_map/dot_general | solution.py:21
  118.1 0.0 copy-done
  118.1 4.9 %convolution_bitcast_fusion = f32[5120,432]{0,1:T(8,128)} fusion(bf16[256,5120]{1,0:T(8,128)(2,1)S(1)} %copy-done, f32[256,432]{0,1:T(8,128)S(1)} %get-tuple-element.5, bf16[256,432]{0,1:T(8,128)(2,1)S(1)} %copy-done.4), kind=kOutput, calls=%fused_computation | convolution fusion | flops 1133236224 | bytes 12132352 | tf_op jit(solution)/shard_map/dot_general | solution.py:30
  123.0 0.0 all-to-all-done
  123.0 1.0 reduce_sum.12
  (3 shorter events, 0.0 us)
Async XLA Ops:
  7.2 44.4 %all-gather.3.cloned.1.call-start = ((), (), s32[]{:S(2)}) async-start(), calls=%async_computation.1 | async-start | bytes 2703360 | tf_op jit(solution)/shard_map/all_gather | solution.py:15
  8.0 98.4 %all-gather.5.cloned.1.call-start = ((), (), s32[]{:S(2)}) async-start(), calls=%async_computation.2 | async-start | bytes 2703360 | tf_op jit(solution)/shard_map/all_gather | solution.py:14
  51.6 4.6 %copy-start.1 = (bf16[5120,432]{0,1:T(8,128)(2,1)S(1)}, bf16[5120,432]{0,1:T(8,128)(2,1)}, u32[]{:S(2)}) copy-start(bf16[5120,432]{0,1:T(8,128)(2,1)} %param.8) | copy-start | bytes 13271044
  56.2 2.3 %copy-start.2 = (bf16[5120,432]{0,1:T(8,128)(2,1)S(1)}, bf16[5120,432]{0,1:T(8,128)(2,1)}, u32[]{:S(2)}) copy-start(bf16[5120,432]{0,1:T(8,128)(2,1)} %param.9) | copy-start | bytes 13271044
  56.2 2.3 %copy-start.4 = (bf16[256,432]{0,1:T(8,128)(2,1)S(1)}, bf16[256,432]{0,1:T(8,128)(2,1)}, u32[]{:S(2)}) copy-start(bf16[256,432]{0,1:T(8,128)(2,1)} %param.11) | copy-start | bytes 663556
  61.7 61.2 %all-to-all-start = ((bf16[32,8,5120]{2,1,0:T(8,128)(2,1)}), bf16[32,8,5120]{2,1,0:T(8,128)(2,1)S(1)}, u32[]{:S(2)}, u32[]{:S(2)}) async-start(bf16[32,8,5120]{2,1,0:T(8,128)(2,1)} %fusion.1), calls=%async_computation | async-start | bytes 5242880 | tf_op jit(solution)/shard_map/all_to_all | solution.py:27
  106.4 6.8 %copy-start.3 = (bf16[256,5120]{1,0:T(8,128)(2,1)S(1)}, bf16[256,5120]{1,0:T(8,128)(2,1)}, u32[]{:S(2)}) copy-start(bf16[256,5120]{1,0:T(8,128)(2,1)} %all-gather.3.cloned.1.call-done) | copy-start | bytes 7864324
  106.4 6.8 %copy-start.5 = (bf16[256,432]{0,1:T(8,128)(2,1)S(1)}, bf16[256,432]{0,1:T(8,128)(2,1)}, u32[]{:S(2)}) copy-start(bf16[256,432]{0,1:T(8,128)(2,1)} %param.12) | copy-start | bytes 663556
  113.1 4.9 %copy-start = (bf16[256,5120]{1,0:T(8,128)(2,1)S(1)}, bf16[256,5120]{1,0:T(8,128)(2,1)}, u32[]{:S(2)}) copy-start(bf16[256,5120]{1,0:T(8,128)(2,1)} %all-gather.5.cloned.1.call-done) | copy-start | bytes 7864324
Sparse Core Ops, SparseCore 0:
  10.1 41.4 all-gather.2
  53.7 52.6 all-gather.4
where the time goes:
time: 133 us; the launch traced here: 131 us
  waiting for transfers between devices  84.2 us (63%)
  matrix products  26.1 us (20%)
  between operations  14.1 us (11%)
  starting transfers between devices  4.78 us (4%)
    all_gather x1, waiting for transfers between devices, local_backward(): dy_full = lax.all_gather(dy_loc, 'tp', axis=0, tiled=True)  42.8 us
    all_gather x1, waiting for transfers between devices, local_backward(): x_full = lax.all_gather(x_loc, 'tp', axis=0, tiled=True)  39.9 us
    dot_general x1, matrix products, local_backward(): lax.dot_general(x_full, d_gate, contract_rows, preferred_element_type=jnp...  6.77 us
    dot_general x1, matrix products, local_backward(): lax.dot_general(z_act, dy_full, contract_rows, preferred_element_type=jnp...  4.93 us
    dot_general x1, matrix products, local_backward(): lax.dot_general(x_full, d_up, contract_rows, preferred_element_type=jnp.f...  4.9 us
    all_to_all x1, starting transfers between devices, local_backward(): received = lax.all_to_all(partial, 'tp', 0, 0, tiled=True)  4.66 us
    dot_general x1, matrix products, local_backward(): lax.dot_general(dy_full, wd_loc, contract_cols, preferred_element_type=jn...  4.61 us
    dot_general x1, matrix products, local_backward(): lax.dot_general(d_up, wu_loc, contract_cols, preferred_element_type=jnp.f...  3.25 us
  transfers between devices with their start and end apart: 3, of which 2 were waited for; matrix products, arithmetic and copies ran while one was open for 20% of the time, Pallas kernels for 0%

commit v1 on v0

v1 whole, which is shorter than its diff:
```python
import math

import jax
import jax.numpy as jnp
from jax import lax
from jax.experimental import pallas as pl
from jax.experimental.pallas import tpu as pltpu
from jax.sharding import PartitionSpec as P

MESH = pl.DeviceIdType.MESH
BF16 = jnp.bfloat16
F32 = jnp.float32
CORES = 2
COL_TILE = 512
VMEM_BYTES = 67043328
NT = (((1,), (1,)), ((), ()))


def comm_kernel(ring, n_copies, x_hbm, dy_hbm, wd_hbm, wg_hbm, wu_hbm, ug_hbm, uu_hbm,
                dx_ref, xf, dyf, dg_t, du_t, z_t,
                wd, wg, wu, ug, uu, gate, up, dgs, dus, pb, pr, sx, sy,
                lf, mg, rw, rm, lf_y, mg_y, rw_y, rm_y, lsem, ssem, rsem):
    R = ring
    me = lax.axis_index("tp")
    c = lax.rem(me, CORES)
    x = lax.rem(me // CORES, R)
    y = me // (CORES * R)
    oc = 1 - c
    rows, hidden = x_hbm.shape
    ch = R * CORES * rows
    H2 = hidden // 2
    LO, HI = pl.ds(0, H2), pl.ds(H2, H2)
    xs = [lax.rem(x + d, R) for d in range(R)]
    ys = [lax.rem(y + d, R) for d in range(R)]

    def dev(yy, xx, cc):
        return {"tp": (yy * R + xx) * CORES + cc}

    xp, xm = dev(y, xs[1], c), dev(y, xs[R - 1], c)
    yp, ym = dev(ys[1], x, c), dev(ys[R - 1], x, c)
    mate = dev(y, x, oc)

    def local(src, dst, i):
        cp = pltpu.make_async_copy(src, dst, lsem.at[i])
        cp.start()
        return cp

    cp_dy = local(dy_hbm, dyf.at[y, x, c], 0)
    cp_x = local(x_hbm, xf.at[y, x, c], 1)
    cp_ug = local(ug_hbm, ug, 2)
    cp_uu = local(uu_hbm, uu, 3)
    cp_wd = local(wd_hbm, wd, 4)
    cp_wg = local(wg_hbm, wg, 5)
    cp_wu = local(wu_hbm, wu, 6)

    barrier = pltpu.get_barrier_semaphore()
    for d in (xp, xm, yp, ym, mate):
        pl.semaphore_signal(barrier, inc=1, device_id=d, device_id_type=MESH)
    pl.semaphore_wait(barrier, 5)

    sent = []

    def send(src, dst, device):
        i = len(sent)
        cp = pltpu.make_async_remote_copy(src_ref=src, dst_ref=dst, send_sem=ssem.at[i], recv_sem=rsem.at[i],
                                          device_id=device, device_id_type=MESH)
        cp.start()
        sent.append(cp)
        return cp

    class Gather:
        def __init__(self, buf):
            self.buf = buf
            self.mate = {}
            self.yp, self.ym, self.yfp, self.yfm = {}, {}, {}, {}

        def to_mate(self, dy_, dx_):
            ref = self.buf.at[ys[dy_], xs[dx_], c]
            self.mate[dy_, dx_] = send(ref, ref, mate)

        def x_send(self):
            ref = self.buf.at[y, x, c]
            self.sp, self.sm = send(ref, ref, xp), send(ref, ref, xm)

        def x_recv_near(self):
            self.sp.wait_recv()
            ref = self.buf.at[y, xs[R - 1], c, :, LO]
            self.fp = send(ref, ref, xp)
            self.sm.wait_recv()
            ref = self.buf.at[y, xs[1], c, :, HI]
            self.fm = send(ref, ref, xm)

        def x_recv_far(self):
            self.fp.wait_recv()
            self.fm.wait_recv()

        def y_send(self, d):
            ref = self.buf.at[y, xs[d], c]
            self.yp[d] = send(ref, ref, yp)
            self.ym[d] = send(ref, ref, ym)

        def y_recv_near(self, d):
            self.yp[d].wait_recv()
            ref = self.buf.at[ys[R - 1], xs[d], c, :, LO]
            self.yfp[d] = send(ref, ref, yp)
            self.ym[d].wait_recv()
            ref = self.buf.at[ys[1], xs[d], c, :, HI]
            self.yfm[d] = send(ref, ref, ym)
            self.to_mate(R - 1, d)
            self.to_mate(1, d)

        def y_recv_far(self, d):
            self.yfp[d].wait_recv()
            self.yfm[d].wait_recv()
            self.to_mate(2, d)

        def mate_recv(self, dy_):
            for d in range(R):
                self.mate[dy_, d].wait_recv()

    gd, gx = Gather(dyf), Gather(xf)
    cp_dy.wait()
    gd.x_send()
    gd.y_send(0)
    gd.to_mate(0, 0)
    cp_x.wait()
    gx.x_send()
    gx.to_mate(0, 0)

    cp_ug.wait()
    cp_uu.wait()
    g_f = ug[...].astype(F32)
    u_f = uu[...].astype(F32)
    z_t[...] = (g_f * jax.nn.sigmoid(g_f) * u_f).astype(BF16)
    gate[...] = g_f.T
    up[...] = u_f.T

    gd.x_recv_near()
    gd.y_send(R - 1)
    gd.y_send(1)
    gd.to_mate(0, R - 1)
    gd.to_mate(0, 1)
    gd.y_recv_near(0)
    gx.x_recv_near()
    gx.to_mate(0, R - 1)
    gx.to_mate(0, 1)
    gd.x_recv_far()
    gd.y_send(2)
    gd.to_mate(0, 2)
    gd.y_recv_near(R - 1)
    gd.y_recv_near(1)
    gx.x_recv_far()
    gx.to_mate(0, 2)

    order = (0, 1, R - 1, 2)

    def grads(k):
        yy = ys[k]
        tok = pl.ds(pl.multiple_of(yy * ch, ch), ch)
        dyc = dyf[yy].reshape(ch, hidden)
        g_mid = lax.dot_general(dyc, wd[...], NT, preferred_element_type=F32)
        g_f, u_f = gate[tok, :], up[tok, :]
        s = jax.nn.sigmoid(g_f)
        dg = (g_mid * u_f * s * (1.0 + g_f * (1.0 - s))).astype(BF16)
        du = (g_mid * (g_f * s)).astype(BF16)
        dgs[tok, :] = dg
        dus[tok, :] = du

    def partial(k, half):
        yy = ys[k]
        tok = pl.ds(pl.multiple_of(yy * ch, ch), ch)
        dg, du = dgs[tok, :], dus[tok, :]

        @pl.loop(0, H2 // COL_TILE)
        def _(t):
            cols = pl.ds(pl.multiple_of(half * H2 + t * COL_TILE, COL_TILE), COL_TILE)
            p = (jnp.dot(dg, wg[:, cols], preferred_element_type=F32)
                 + jnp.dot(du, wu[:, cols], preferred_element_type=F32))
            pb[k, :, :, :, cols] = p.astype(BF16).reshape(R, CORES, rows, COL_TILE)

        cols = (LO, HI)[half]
        return send(pb.at[k, :, oc, :, cols], pr.at[k, :, :, cols], mate)

    def pair_sum(k, half, cp):
        cp.wait_recv()
        cols = (LO, HI)[half]
        for j in range(R):
            sx[k, j, :, cols] = pb[k, j, c, :, cols].astype(F32) + pr[k, j, :, cols].astype(F32)

    leaf, raw, merged = {}, {}, {}

    def scatter_first(k):
        leaf[k] = (send(sx.at[k, xs[2], :, LO], lf.at[k, 0], xp), send(sx.at[k, xs[2], :, HI], lf.at[k, 1], xm))
        raw[k] = (send(sx.at[k, xs[1], :, HI], rw.at[k, 0], xp), send(sx.at[k, xs[R - 1], :, LO], rw.at[k, 1], xm))

    def scatter_merge(k):
        leaf[k][0].wait_recv()
        mg[k, 0] = lf[k, 0] + sx[k, xs[1], :, LO]
        a = send(mg.at[k, 0], rm.at[k, 0], xp)
        leaf[k][1].wait_recv()
        mg[k, 1] = lf[k, 1] + sx[k, xs[R - 1], :, HI]
        merged[k] = (a, send(mg.at[k, 1], rm.at[k, 1], xm))

    def scatter_last(k):
        for cp in raw[k] + merged[k]:
            cp.wait_recv()
        sy[k, :, LO] = sx[k, x, :, LO] + rm[k, 0] + rw[k, 1]
        sy[k, :, HI] = sx[k, x, :, HI] + rw[k, 0] + rm[k, 1]

    gd.mate_recv(0)
    cp_wd.wait()
    grads(0)
    gd.y_recv_near(2)
    cp_wg.wait()
    cp_wu.wait()
    p0 = partial(0, 0)
    gd.y_recv_far(0)
    gd.y_recv_far(R - 1)
    gd.y_recv_far(1)
    p1 = partial(0, 1)
    pair_sum(0, 0, p0)
    pair_sum(0, 1, p1)
    scatter_first(0)
    gd.y_recv_far(2)
    for d in (0, R - 1, 1, 2):
        gx.y_send(d)
    gd.mate_recv(1)
    grads(1)
    p0 = partial(1, 0)
    scatter_merge(0)
    p1 = partial(1, 1)
    pair_sum(1, 0, p0)
    pair_sum(1, 1, p1)
    scatter_first(1)
    gd.mate_recv(R - 1)
    grads(R - 1)
    p0 = partial(R - 1, 0)
    gx.y_recv_near(0)
    scatter_last(0)
    scatter_merge(1)
    p1 = partial(R - 1, 1)
    pair_sum(R - 1, 0, p0)
    pair_sum(R - 1, 1, p1)
    scatter_first(R - 1)
    gx.y_recv_near(R - 1)
    gd.mate_recv(2)
    grads(2)
    p0 = partial(2, 0)
    gx.y_recv_near(1)
    scatter_merge(R - 1)
    p1 = partial(2, 1)
    pair_sum(2, 0, p0)
    pair_sum(2, 1, p1)
    scatter_first(2)
    gx.y_recv_near(2)
    dg_t[...] = dgs[...].astype(F32).T.astype(BF16)
    du_t[...] = dus[...].astype(F32).T.astype(BF16)
    scatter_last(1)
    raw_p = send(sy.at[1, :, HI], rw_y.at[0], yp)
    scatter_merge(2)
    scatter_last(R - 1)
    raw_m = send(sy.at[R - 1, :, LO], rw_y.at[1], ym)
    for d in (0, R - 1, 1, 2):
        gx.y_recv_far(d)
    scatter_last(2)
    leaf_p = send(sy.at[2, :, LO], lf_y.at[0], yp)
    leaf_m = send(sy.at[2, :, HI], lf_y.at[1], ym)
    leaf_p.wait_recv()
    mg_y[0] = lf_y[0] + sy[1, :, LO]
    mp = send(mg_y.at[0], rm_y.at[0], yp)
    leaf_m.wait_recv()
    mg_y[1] = lf_y[1] + sy[R - 1, :, HI]
    mm = send(mg_y.at[1], rm_y.at[1], ym)
    for k in range(R):
        gx.mate_recv(k)
    for cp in (raw_p, raw_m, mp, mm):
        cp.wait_recv()
    dx_ref[:, LO] = (sy[0, :, LO] + rm_y[0] + rw_y[1]).astype(BF16)
    dx_ref[:, HI] = (sy[0, :, HI] + rw_y[0] + rm_y[1]).astype(BF16)
    for cp in sent:
        cp.wait_send()
    assert len(sent) == n_copies, len(sent)


def weight_kernel(xf, dyf, dg_t, du_t, z_t, og, ou, od):
    tile = og.shape[1]
    tokens = dg_t.shape[1]
    cols = pl.ds(pl.multiple_of(pl.program_id(0) * tile, tile), tile)
    xc = xf[:, :, :, :, cols].reshape(tokens, tile)
    og[...] = jnp.dot(dg_t[...], xc, preferred_element_type=F32)
    ou[...] = jnp.dot(du_t[...], xc, preferred_element_type=F32)
    od[...] = jnp.dot(z_t[...], dyf[:, :, :, :, cols].reshape(tokens, tile), preferred_element_type=F32)


def solution(mesh):
    tp = mesh.shape["tp"]
    ring = math.isqrt(tp // CORES)

    def local_backward(x_loc, wg_loc, wu_loc, wd_loc, ug_loc, uu_loc, dy_loc):
        rows, hidden = x_loc.shape
        ffn = wd_loc.shape[0]
        tokens = tp * rows
        H2 = hidden // 2
        R = ring
        n_copies = 2 * (4 + 4 * R + R * R) + 8 * R + 6
        full = (R, R, CORES, rows, hidden)
        half = (rows, H2)
        vm = pltpu.VMEM
        out_bytes = 2 * (rows * hidden + 2 * tokens * hidden + 3 * ffn * tokens)
        dx, xf, dyf, dg_t, du_t, z_t = pl.pallas_call(
            lambda *refs: comm_kernel(R, n_copies, *refs),
            name="comm",
            out_shape=(vm((rows, hidden), BF16), vm(full, BF16), vm(full, BF16),
                       vm((ffn, tokens), BF16), vm((ffn, tokens), BF16), vm((ffn, tokens), BF16)),
            in_specs=[pl.BlockSpec(memory_space=pltpu.HBM)] * 7,
            out_specs=(pl.BlockSpec(memory_space=vm),) * 6,
            scratch_shapes=[
                vm((ffn, hidden), BF16), vm((ffn, hidden), BF16), vm((ffn, hidden), BF16),
                vm((ffn, tokens), BF16), vm((ffn, tokens), BF16),
                vm((tokens, ffn), F32), vm((tokens, ffn), F32),
                vm((tokens, ffn), BF16), vm((tokens, ffn), BF16),
                vm((R,) + full[1:], BF16), vm((R, R, rows, hidden), BF16),
                vm((R, R, rows, hidden), F32), vm((R, rows, hidden), F32),
                vm((R, 2) + half, F32), vm((R, 2) + half, F32), vm((R, 2) + half, F32), vm((R, 2) + half, F32),
                vm((2,) + half, F32), vm((2,) + half, F32), vm((2,) + half, F32), vm((2,) + half, F32),
                pltpu.SemaphoreType.DMA((7,)),
                pltpu.SemaphoreType.DMA((n_copies,)),
                pltpu.SemaphoreType.DMA((n_copies,)),
            ],
            compiler_params=pltpu.CompilerParams(collective_id=0, has_side_effects=True, vmem_limit_bytes=VMEM_BYTES - out_bytes - 40960),
        )(x_loc, dy_loc, wd_loc, wg_loc.T, wu_loc.T, ug_loc.T, uu_loc.T)
        out = jax.ShapeDtypeStruct((ffn, hidden), F32)
        ospec = pl.BlockSpec((ffn, COL_TILE), lambda j: (0, j))
        gw_g, gw_u, gw_d = pl.pallas_call(
            weight_kernel,
            name="weight_grads",
            grid=(hidden // COL_TILE,),
            out_shape=(out, out, out),
            in_specs=[pl.BlockSpec(memory_space=vm)] * 5,
            out_specs=(ospec, ospec, ospec),
            compiler_params=pltpu.CompilerParams(vmem_limit_bytes=24 << 20),
        )(xf, dyf, dg_t, du_t, z_t)
        return dx, gw_g.T, gw_u.T, gw_d

    row_spec = P(("dp", "tp"), None)
    col_spec = P(None, "tp")
    part_cols = P("dp", "tp")
    return jax.shard_map(local_backward, mesh=mesh,
                         in_specs=(row_spec, col_spec, col_spec, P("tp", None), part_cols, part_cols, row_spec),
                         out_specs=(row_spec, part_cols, part_cols, row_spec),
                         check_vma=False)
```

time: 133 us -> 73.1 us (0.55)
  waiting for transfers between devices: 84.2 us -> 0 us
  Pallas kernels: 0 us -> 71 us
  matrix products: 26.1 us -> 0 us
  between operations: 14.1 us -> 0.64 us
  starting transfers between devices: 4.78 us -> 0 us
    all_gather x2 -> x0, waiting for transfers between devices: 82.8 us -> none  [the longest x1 42.8 us: local_backward(): dy_full = lax.all_gather(dy_loc, 'tp', axis=0, tiled=True)]
    pallas_call x0 -> x2, Pallas kernels: none -> 71 us  [the longest x1 60.8 us: local_backward(): pl.pallas_call(lambda *refs: comm_kernel(R, n_copies, *refs), name='comm'...]
    dot_general x6 -> x0, matrix products: 26.1 us -> none  [the longest x1 6.77 us: local_backward(): lax.dot_general(x_full, d_gate, contract_rows, preferred_element_type=jnp...]
    all_to_all x1 -> x0, starting transfers between devices: 4.66 us -> none  [local_backward(): received = lax.all_to_all(partial, 'tp', 0, 0, tiled=True)]
    unnamed x2 -> x0, waiting for transfers between devices: 1.45 us -> none
  transfers between devices with their start and end apart: 3 -> 0, of which waited for: 2 -> 0; matrix products, arithmetic and copies ran while one was open for 20% -> 0% of each run, Pallas kernels for 0% -> 0%
where the time goes in v1:
time: 73.1 us; the launch traced here: 72.2 us
  Pallas kernels  71 us (97%)
    pallas_call x1, Pallas kernels, local_backward(): pl.pallas_call(lambda *refs: comm_kernel(R, n_copies, *refs), name='comm'...  60.8 us
    pallas_call x1, Pallas kernels, local_backward(): pl.pallas_call(weight_kernel, name='weight_grads', grid=(hidden // COL_TI...  10.1 us

profile of v1, /device:TPU:96, one launch (start us, length us, event | category | flops | bytes accessed | tf_op | source)
XLA Modules:
  0.0 72.2 jit_solution(5677240144730551080)
XLA Ops:
  0.6 60.8 %comm.1 = (bf16[8,5120]{1,0:T(8,128)(2,1)S(1)}, bf16[4,4,2,8,5120]{4,3,2,1,0:T(8,128)(2,1)S(1)}, bf16[4,4,2,8,5120]{4,3,2,1,0:T(8,128)(2,1)S(1)}, bf16[432,256]{...) custom-call(bf16[8,5120]{1,0:T(8,128)(2,1)} %refs_0_.1, bf16[8,5120]{1,0:T(8,128)(2,1)} %refs_1_.1, ...), custom_call_target="tpu_custom_call" | custom-call | tf_op jit(solution)/shard_map/comm/pallas_call | solution.py:310
  61.5 0.6 copy.12
  62.1 10.1 %weight_grads.1 = (f32[432,5120]{1,0:T(8,128)}, f32[432,5120]{1,0:T(8,128)}, f32[432,5120]{1,0:T(8,128)}) custom-call(bf16[4,4,2,8,5120]{4,3,2,1,0:T(8,128)(2,1)S(1)} %get-tuple-element.14.xf, bf16[4,4,2,8,5120]{4,3,2,1,0:T(8,128)(2,1)S(1)} %get-tuple-element.15.dyf, bf16[432,256]{1,0:T(8,128)(2,1)S(1)} %get-tuple-element.16.dg_t, ...), custom_call_target="tpu_custom_call" | custom-call | tf_op jit(solution)/shard_map/weight_grads/pallas_call | solution.py:334

commit v2 on v0

v2 whole, which is shorter than its diff:
```python
import math

import jax
import jax.numpy as jnp
from jax import lax
from jax.experimental import pallas as pl
from jax.experimental.pallas import tpu as pltpu
from jax.sharding import PartitionSpec as P

MESH = pl.DeviceIdType.MESH
BF16 = jnp.bfloat16
F32 = jnp.float32
CORES = 2
COL_TILE = 512
MXU_TILE = 256
GROUPS = 2
VMEM_BYTES = 67043328
NT = (((1,), (1,)), ((), ()))


def comm_kernel(ring, n_copies, x_hbm, dy_hbm, wd_hbm, wg_hbm, wu_hbm, ug_hbm, uu_hbm,
                dx_ref, xf, dyf, dg_t, du_t, z_t,
                wd, wg, wu, ug, uu, gate, up, mid, dgs, dus, pb, pr, sx, sy,
                lf, mg, rw, rm, lf2, mg2, rw2, rm2, lsem, ssem, rsem):
    R = ring
    me = lax.axis_index("tp")
    c = lax.rem(me, CORES)
    x = lax.rem(me // CORES, R)
    y = me // (CORES * R)
    oc = 1 - c
    rows, hidden = x_hbm.shape
    tokens = R * R * CORES * rows
    H2, Q = hidden // 2, hidden // 4
    xs = [lax.rem(x + d, R) for d in range(R)]
    ys = [lax.rem(y + d, R) for d in range(R)]

    def dev(yy, xx, cc):
        return {"tp": (yy * R + xx) * CORES + cc}

    nbr = {(0, 1): dev(y, xs[1], c), (0, -1): dev(y, xs[R - 1], c),
           (1, 1): dev(ys[1], x, c), (1, -1): dev(ys[R - 1], x, c)}
    mate = dev(y, x, oc)

    def local(src, dst, i):
        cp = pltpu.make_async_copy(src, dst, lsem.at[i])
        cp.start()
        return cp

    cp_dy = local(dy_hbm, dyf.at[y, x, c], 0)
    cp_x = local(x_hbm, xf.at[y, x, c], 1)
    cp_ug = local(ug_hbm, ug, 2)
    cp_uu = local(uu_hbm, uu, 3)
    cp_wd = local(wd_hbm, wd, 4)
    cp_wg = local(wg_hbm, wg, 5)
    cp_wu = local(wu_hbm, wu, 6)

    barrier = pltpu.get_barrier_semaphore()
    for d in (*nbr.values(), mate):
        pl.semaphore_signal(barrier, inc=1, device_id=d, device_id_type=MESH)
    pl.semaphore_wait(barrier, 5)

    sent = []

    def send(src, dst, device):
        i = len(sent)
        cp = pltpu.make_async_remote_copy(src_ref=src, dst_ref=dst, send_sem=ssem.at[i], recv_sem=rsem.at[i],
                                          device_id=device, device_id_type=MESH)
        cp.start()
        sent.append(cp)
        return cp

    class Half:
        def __init__(self, buf, first):
            self.buf, self.first = buf, first
            base = first * H2
            self.all, self.lo, self.hi = pl.ds(base, H2), pl.ds(base, Q), pl.ds(base + Q, Q)
            self.near, self.far, self.rows = {}, {}, {}

        def ref(self, d1, d2, cols):
            if self.first == 0:
                return self.buf.at[ys[d2], xs[d1], c, :, cols]
            return self.buf.at[ys[d1], xs[d2], c, :, cols]

        def push(self, key, d1, d2, axis):
            ref = self.ref(d1, d2, self.all)
            self.near[key] = (send(ref, ref, nbr[axis, 1]), send(ref, ref, nbr[axis, -1]))

        def relay(self, key, minus, plus, axis):
            self.near[key][0].wait_recv()
            ref = self.ref(*minus, self.lo)
            a = send(ref, ref, nbr[axis, 1])
            self.near[key][1].wait_recv()
            ref = self.ref(*plus, self.hi)
            self.far[key] = (a, send(ref, ref, nbr[axis, -1]))

        def first_send(self):
            self.push("f", 0, 0, self.first)

        def first_relay(self):
            self.relay("f", (R - 1, 0), (1, 0), self.first)

        def first_far(self):
            for cp in self.far["f"]:
                cp.wait_recv()

        def second_send(self, d1):
            self.push(d1, d1, 0, 1 - self.first)

        def second_relay(self, d1):
            self.relay(d1, (d1, R - 1), (d1, 1), 1 - self.first)

        def second_far(self, d1):
            for cp in self.far[d1]:
                cp.wait_recv()

        def to_mate(self, d2):
            if self.first == 0:
                ref = self.buf.at[ys[d2], :, c, :, self.all]
            else:
                ref = self.buf.at[:, xs[d2], c, :, self.all]
            self.rows[d2] = send(ref, ref, mate)

        def mate_recv(self):
            for cp in self.rows.values():
                cp.wait_recv()

    class Gather:
        def __init__(self, buf):
            self.halves = (Half(buf, 0), Half(buf, 1))

        def __getattr__(self, name):
            def both(*args):
                for h in self.halves:
                    getattr(h, name)(*args)
            return both

    def prepare():
        g_f = ug[...].astype(F32)
        u_f = uu[...].astype(F32)
        z_t[...] = (g_f * jax.nn.sigmoid(g_f) * u_f).astype(BF16)
        gate[...] = g_f.T
        up[...] = u_f.T

    def grads():
        mid[...] = lax.dot_general(dyf[...].reshape(tokens, hidden), wd[...], NT, preferred_element_type=F32)
        step = tokens // 8
        for i in range(8):
            tok = pl.ds(i * step, step)
            g_mid, g_f, u_f = mid[tok, :], gate[tok, :], up[tok, :]
            s = jax.nn.sigmoid(g_f)
            dgs[tok, :] = (g_mid * u_f * s * (1.0 + g_f * (1.0 - s))).astype(BF16)
            dus[tok, :] = (g_mid * (g_f * s)).astype(BF16)

    kinds = ((0, 1, 0), (1, 1, H2), (0, -1, Q), (1, -1, H2 + Q))
    W = Q // GROUPS
    pair, leaf, raw, merged, leaf2, raw2, merged2 = {}, {}, {}, {}, {}, {}, {}

    def piece_cols(n, g):
        return pl.ds(kinds[n][2] + g * W, W)

    def partial(n):
        dg, du = dgs[...], dus[...]
        for t in range(Q // MXU_TILE):
            cols = pl.ds(kinds[n][2] + t * MXU_TILE, MXU_TILE)
            p = (jnp.dot(dg, wg[:, cols], preferred_element_type=F32)
                 + jnp.dot(du, wu[:, cols], preferred_element_type=F32))
            pb[:, :, :, :, cols] = p.astype(BF16).reshape(R, R, CORES, rows, MXU_TILE)
        for g in range(GROUPS):
            cols = piece_cols(n, g)
            pair[n, g] = send(pb.at[:, :, oc, :, cols], pr.at[:, :, :, cols], mate)

    def line(n, d, cols):
        if kinds[n][0] == 0:
            return sx.at[:, xs[d], :, cols]
        return sx.at[ys[d], :, :, cols]

    def spot(n, d):
        return (ys if kinds[n][0] == 0 else xs)[d]

    def scatter_first(n, g):
        axis, s, _ = kinds[n]
        cols = piece_cols(n, g)
        pair[n, g].wait_recv()
        for yy in range(R):
            sx[yy, :, :, cols] = pb[yy, :, c, :, cols].astype(F32) + pr[yy, :, :, cols].astype(F32)
        leaf[n, g] = send(line(n, 2, cols), lf.at[:, :, cols], nbr[axis, s])
        raw[n, g] = send(line(n, -s % R, cols), rw.at[:, :, cols], nbr[axis, -s])

    def scatter_merge(n, g):
        axis, s, _ = kinds[n]
        cols = piece_cols(n, g)
        leaf[n, g].wait_recv()
        mg[:, :, cols] = lf[:, :, cols] + line(n, s % R, cols)[...]
        merged[n, g] = send(mg.at[:, :, cols], rm.at[:, :, cols], nbr[axis, s])

    def scatter_second(n, g):
        axis, s, _ = kinds[n]
        cols = piece_cols(n, g)
        raw[n, g].wait_recv()
        merged[n, g].wait_recv()
        sy[:, :, cols] = line(n, 0, cols)[...] + rm[:, :, cols] + rw[:, :, cols]
        leaf2[n, g] = send(sy.at[spot(n, 2), :, cols], lf2.at[:, cols], nbr[1 - axis, s])
        raw2[n, g] = send(sy.at[spot(n, -s % R), :, cols], rw2.at[:, cols], nbr[1 - axis, -s])

    def scatter_merge2(n, g):
        axis, s, _ = kinds[n]
        cols = piece_cols(n, g)
        leaf2[n, g].wait_recv()
        mg2[:, cols] = lf2[:, cols] + sy[spot(n, s % R), :, cols]
        merged2[n, g] = send(mg2.at[:, cols], rm2.at[:, cols], nbr[1 - axis, s])

    def scatter_last(n, g):
        cols = piece_cols(n, g)
        raw2[n, g].wait_recv()
        merged2[n, g].wait_recv()
        dx_ref[:, cols] = (sy[spot(n, 0), :, cols] + rm2[:, cols] + rw2[:, cols]).astype(BF16)

    def pieces(f, g):
        for n in range(len(kinds)):
            f(n, g)

    def transposes():
        dg_t[...] = dgs[...].astype(F32).T.astype(BF16)
        du_t[...] = dus[...].astype(F32).T.astype(BF16)

    gd, gx = Gather(dyf), Gather(xf)
    cp_dy.wait()
    gd.first_send()
    gd.second_send(0)
    cp_x.wait()
    cp_ug.wait()
    cp_uu.wait()
    prepare()
    gd.first_relay()
    gd.second_send(R - 1)
    gd.second_send(1)
    gx.first_send()
    gd.second_relay(0)
    gd.first_far()
    gd.second_send(2)
    gd.to_mate(0)
    gd.second_relay(R - 1)
    gd.second_relay(1)
    gx.first_relay()
    gx.second_send(0)
    gd.second_relay(2)
    gd.to_mate(R - 1)
    gd.to_mate(1)
    gx.second_send(R - 1)
    gx.second_send(1)
    gx.first_far()
    gx.second_send(2)
    gx.to_mate(0)
    gd.second_far(0)
    gd.second_far(R - 1)
    gd.second_far(1)
    gd.second_far(2)
    gd.to_mate(2)
    gx.second_relay(0)
    cp_wd.wait()
    gd.mate_recv()
    grads()
    gx.second_relay(R - 1)
    gx.second_relay(1)
    cp_wg.wait()
    cp_wu.wait()
    partial(0)
    partial(1)
    scatter_first(0, 0)
    partial(2)
    scatter_first(1, 0)
    gx.second_relay(2)
    partial(3)
    scatter_first(2, 0)
    scatter_first(3, 0)
    gx.to_mate(R - 1)
    gx.to_mate(1)
    for g in range(1, GROUPS):
        pieces(scatter_first, g)
    pieces(scatter_merge, 0)
    transposes()
    gx.second_far(0)
    gx.second_far(R - 1)
    gx.second_far(1)
    gx.second_far(2)
    gx.to_mate(2)
    pieces(scatter_merge, 1)
    pieces(scatter_second, 0)
    pieces(scatter_second, 1)
    pieces(scatter_merge2, 0)
    pieces(scatter_merge2, 1)
    gx.mate_recv()
    pieces(scatter_last, 0)
    pieces(scatter_last, 1)
    for cp in sent:
        cp.wait_send()
    assert len(sent) == n_copies, len(sent)


def weight_kernel(xf, dyf, dg_t, du_t, z_t, dx, og, ou, od, odx):
    tile = og.shape[1]
    tokens = dg_t.shape[1]
    cols = pl.ds(pl.multiple_of(pl.program_id(0) * tile, tile), tile)
    xc = xf[:, :, :, :, cols].reshape(tokens, tile)
    og[...] = jnp.dot(dg_t[...], xc, preferred_element_type=F32)
    ou[...] = jnp.dot(du_t[...], xc, preferred_element_type=F32)
    od[...] = jnp.dot(z_t[...], dyf[:, :, :, :, cols].reshape(tokens, tile), preferred_element_type=F32)
    odx[...] = dx[:, cols]


def solution(mesh):
    tp = mesh.shape["tp"]
    ring = math.isqrt(tp // CORES)

    def local_backward(x_loc, wg_loc, wu_loc, wd_loc, ug_loc, uu_loc, dy_loc):
        rows, hidden = x_loc.shape
        ffn = wd_loc.shape[0]
        tokens = tp * rows
        R = ring
        n_copies = 2 * 2 * (4 + 4 * R + R) + 4 * GROUPS * 7
        full = (R, R, CORES, rows, hidden)
        vm = pltpu.VMEM
        out_bytes = 2 * (rows * hidden + 2 * tokens * hidden + 3 * ffn * tokens)
        dx, xf, dyf, dg_t, du_t, z_t = pl.pallas_call(
            lambda *refs: comm_kernel(R, n_copies, *refs),
            name="comm",
            out_shape=(vm((rows, hidden), BF16), vm(full, BF16), vm(full, BF16),
                       vm((ffn, tokens), BF16), vm((ffn, tokens), BF16), vm((ffn, tokens), BF16)),
            in_specs=[pl.BlockSpec(memory_space=pltpu.HBM)] * 7,
            out_specs=(pl.BlockSpec(memory_space=vm),) * 6,
            scratch_shapes=[
                vm((ffn, hidden), BF16), vm((ffn, hidden), BF16), vm((ffn, hidden), BF16),
                vm((ffn, tokens), BF16), vm((ffn, tokens), BF16),
                vm((tokens, ffn), F32), vm((tokens, ffn), F32), vm((tokens, ffn), F32),
                vm((tokens, ffn), BF16), vm((tokens, ffn), BF16),
                vm(full, BF16), vm((R, R, rows, hidden), BF16),
                vm((R, R, rows, hidden), F32), vm((R, rows, hidden), F32),
                *[vm((R, rows, hidden), F32)] * 4, *[vm((rows, hidden), F32)] * 4,
                pltpu.SemaphoreType.DMA((7,)),
                pltpu.SemaphoreType.DMA((n_copies,)),
                pltpu.SemaphoreType.DMA((n_copies,)),
            ],
            compiler_params=pltpu.CompilerParams(collective_id=0, has_side_effects=True,
                                                 vmem_limit_bytes=VMEM_BYTES - out_bytes - 40960),
        )(x_loc, dy_loc, wd_loc, wg_loc.T, wu_loc.T, ug_loc.T, uu_loc.T)
        out = jax.ShapeDtypeStruct((ffn, hidden), F32)
        ospec = pl.BlockSpec((ffn, COL_TILE), lambda j: (0, j))
        gw_g, gw_u, gw_d, dx = pl.pallas_call(
            weight_kernel,
            name="weight_grads",
            grid=(hidden // COL_TILE,),
            out_shape=(out, out, out, jax.ShapeDtypeStruct((rows, hidden), BF16)),
            in_specs=[pl.BlockSpec(memory_space=vm)] * 6,
            out_specs=(ospec, ospec, ospec, pl.BlockSpec((rows, COL_TILE), lambda j: (0, j))),
            compiler_params=pltpu.CompilerParams(vmem_limit_bytes=24 << 20),
        )(xf, dyf, dg_t, du_t, z_t, dx)
        return dx, gw_g.T, gw_u.T, gw_d

    row_spec = P(("dp", "tp"), None)
    col_spec = P(None, "tp")
    part_cols = P("dp", "tp")
    return jax.shard_map(local_backward, mesh=mesh,
                         in_specs=(row_spec, col_spec, col_spec, P("tp", None), part_cols, part_cols, row_spec),
                         out_specs=(row_spec, part_cols, part_cols, row_spec),
                         check_vma=False)
```

time: 133 us -> 60.5 us (0.45); the launches traced: 131 us -> 60 us
  waiting for transfers between devices: 84.2 us -> 0 us
  Pallas kernels: 0 us -> 59.4 us
  matrix products: 26.1 us -> 0 us
  between operations: 14.1 us -> 0.64 us
  starting transfers between devices: 4.78 us -> 0 us
    all_gather x2 -> x0, waiting for transfers between devices: 82.8 us -> none  [the longest x1 42.8 us: local_backward(): dy_full = lax.all_gather(dy_loc, 'tp', axis=0, tiled=True)]
    pallas_call x0 -> x2, Pallas kernels: none -> 59.4 us  [the longest x1 49.2 us: local_backward(): pl.pallas_call(lambda *refs: comm_kernel(R, n_copies, *refs), name='comm'...]
    dot_general x6 -> x0, matrix products: 26.1 us -> none  [the longest x1 6.77 us: local_backward(): lax.dot_general(x_full, d_gate, contract_rows, preferred_element_type=jnp...]
    all_to_all x1 -> x0, starting transfers between devices: 4.66 us -> none  [local_backward(): received = lax.all_to_all(partial, 'tp', 0, 0, tiled=True)]
    unnamed x2 -> x0, waiting for transfers between devices: 1.45 us -> none
  transfers between devices with their start and end apart: 3 -> 0, of which waited for: 2 -> 0; matrix products, arithmetic and copies ran while one was open for 20% -> 0% of each run, Pallas kernels for 0% -> 0%
where the time goes in v2:
time: 60.5 us; the launch traced here: 60 us
  Pallas kernels  59.4 us (98%)
  between operations  0.64 us (1%)
    pallas_call x1, Pallas kernels, local_backward(): pl.pallas_call(lambda *refs: comm_kernel(R, n_copies, *refs), name='comm'...  49.2 us
    pallas_call x1, Pallas kernels, local_backward(): pl.pallas_call(weight_kernel, name='weight_grads', grid=(hidden // COL_TI...  10.2 us

profile of v2, /device:TPU:96, one launch (start us, length us, event | category | flops | bytes accessed | tf_op | source)
XLA Modules:
  0.0 60.0 jit_solution(12938744880281743850)
XLA Ops:
  0.6 49.2 %comm.1 = (bf16[8,5120]{1,0:T(8,128)(2,1)S(1)}, bf16[4,4,2,8,5120]{4,3,2,1,0:T(8,128)(2,1)S(1)}, bf16[4,4,2,8,5120]{4,3,2,1,0:T(8,128)(2,1)S(1)}, bf16[432,256]{...) custom-call(bf16[8,5120]{1,0:T(8,128)(2,1)} %refs_0_.1, bf16[8,5120]{1,0:T(8,128)(2,1)} %refs_1_.1, ...), custom_call_target="tpu_custom_call" | custom-call | tf_op jit(solution)/shard_map/comm/pallas_call | solution.py:324
  49.8 10.2 %weight_grads.1 = (f32[432,5120]{1,0:T(8,128)}, f32[432,5120]{1,0:T(8,128)}, f32[432,5120]{1,0:T(8,128)}, bf16[8,5120]{1,0:T(8,128)(2,1)}) custom-call(bf16[4,4,2,8,5120]{4,3,2,1,0:T(8,128)(2,1)S(1)} %get-tuple-element.14.xf, bf16[4,4,2,8,5120]{4,3,2,1,0:T(8,128)(2,1)S(1)} %get-tuple-element.15.dyf, bf16[432,256]{1,0:T(8,128)(2,1)S(1)} %get-tuple-element.16.dg_t, ...), custom_call_target="tpu_custom_call" | custom-call | tf_op jit(solution)/shard_map/weight_grads/pallas_call | solution.py:348

commit v3 on v2

--- a/solution.py
+++ b/solution.py
@@ -11,9 +11,9 @@
 BF16 = jnp.bfloat16
 F32 = jnp.float32
 CORES = 2
-COL_TILE = 512
+COL_TILE = 1024
 MXU_TILE = 256
-GROUPS = 2
+GROUPS = (2, 2, 1)
 VMEM_BYTES = 67043328
 NT = (((1,), (1,)), ((), ()))
 
@@ -38,7 +38,8 @@
         return {"tp": (yy * R + xx) * CORES + cc}
 
     nbr = {(0, 1): dev(y, xs[1], c), (0, -1): dev(y, xs[R - 1], c),
-           (1, 1): dev(ys[1], x, c), (1, -1): dev(ys[R - 1], x, c)}
+           (1, 1): dev(ys[1], x, c), (1, -1): dev(ys[R - 1], x, c),
+           (0, 2): dev(y, xs[2], c), (1, 2): dev(ys[2], x, c)}
     mate = dev(y, x, oc)
 
     def local(src, dst, i):
@@ -57,7 +58,7 @@
     barrier = pltpu.get_barrier_semaphore()
     for d in (*nbr.values(), mate):
         pl.semaphore_signal(barrier, inc=1, device_id=d, device_id_type=MESH)
-    pl.semaphore_wait(barrier, 5)
+    pl.semaphore_wait(barrier, len(nbr) + 1)
 
     sent = []
 
@@ -103,6 +104,15 @@
             for cp in self.far["f"]:
                 cp.wait_recv()
 
+        def first_direct(self):
+            self.push("f", 0, 0, self.first)
+            ref = self.ref(0, 0, self.all)
+            self.far["f"] = (send(ref, ref, nbr[self.first, 2]),)
+
+        def first_near(self):
+            for cp in self.near["f"]:
+                cp.wait_recv()
+
         def second_send(self, d1):
             self.push(d1, d1, 0, 1 - self.first)
 
@@ -119,6 +129,10 @@
             else:
                 ref = self.buf.at[:, xs[d2], c, :, self.all]
             self.rows[d2] = send(ref, ref, mate)
+
+        def spot_to_mate(self, d1, d2):
+            ref = self.ref(d1, d2, self.all)
+            self.rows[d1, d2] = send(ref, ref, mate)
 
         def mate_recv(self):
             for cp in self.rows.values():
@@ -152,22 +166,22 @@
             dus[tok, :] = (g_mid * (g_f * s)).astype(BF16)
 
     kinds = ((0, 1, 0), (1, 1, H2), (0, -1, Q), (1, -1, H2 + Q))
-    W = Q // GROUPS
+    widths = [t * MXU_TILE for t in GROUPS]
+    starts = [sum(widths[:g]) for g in range(len(widths))]
     pair, leaf, raw, merged, leaf2, raw2, merged2 = {}, {}, {}, {}, {}, {}, {}
 
     def piece_cols(n, g):
-        return pl.ds(kinds[n][2] + g * W, W)
-
-    def partial(n):
+        return pl.ds(kinds[n][2] + starts[g], widths[g])
+
+    def partial(n, g):
         dg, du = dgs[...], dus[...]
-        for t in range(Q // MXU_TILE):
-            cols = pl.ds(kinds[n][2] + t * MXU_TILE, MXU_TILE)
+        for t in range(GROUPS[g]):
+            cols = pl.ds(kinds[n][2] + starts[g] + t * MXU_TILE, MXU_TILE)
             p = (jnp.dot(dg, wg[:, cols], preferred_element_type=F32)
                  + jnp.dot(du, wu[:, cols], preferred_element_type=F32))
             pb[:, :, :, :, cols] = p.astype(BF16).reshape(R, R, CORES, rows, MXU_TILE)
-        for g in range(GROUPS):
-            cols = piece_cols(n, g)
-            pair[n, g] = send(pb.at[:, :, oc, :, cols], pr.at[:, :, :, cols], mate)
+        cols = piece_cols(n, g)
+        pair[n, g] = send(pb.at[:, :, oc, :, cols], pr.at[:, :, :, cols], mate)
 
     def line(n, d, cols):
         if kinds[n][0] == 0:
@@ -184,6 +198,10 @@
         for yy in range(R):
             sx[yy, :, :, cols] = pb[yy, :, c, :, cols].astype(F32) + pr[yy, :, :, cols].astype(F32)
         leaf[n, g] = send(line(n, 2, cols), lf.at[:, :, cols], nbr[axis, s])
+
+    def scatter_raw(n, g):
+        axis, s, _ = kinds[n]
+        cols = piece_cols(n, g)
         raw[n, g] = send(line(n, -s % R, cols), rw.at[:, :, cols], nbr[axis, -s])
 
     def scatter_merge(n, g):
@@ -225,37 +243,40 @@
 
     gd, gx = Gather(dyf), Gather(xf)
     cp_dy.wait()
-    gd.first_send()
+    gd.first_direct()
     gd.second_send(0)
     cp_x.wait()
     cp_ug.wait()
     cp_uu.wait()
     prepare()
-    gd.first_relay()
+    gd.first_near()
     gd.second_send(R - 1)
     gd.second_send(1)
-    gx.first_send()
-    gd.second_relay(0)
     gd.first_far()
     gd.second_send(2)
+    gd.second_relay(0)
     gd.to_mate(0)
+    gx.first_send()
     gd.second_relay(R - 1)
     gd.second_relay(1)
-    gx.first_relay()
     gx.second_send(0)
     gd.second_relay(2)
     gd.to_mate(R - 1)
     gd.to_mate(1)
+    gd.second_far(0)
+    gd.spot_to_mate(0, 2)
+    gx.first_relay()
     gx.second_send(R - 1)
     gx.second_send(1)
+    gd.second_far(R - 1)
+    gd.spot_to_mate(R - 1, 2)
+    gd.second_far(1)
+    gd.spot_to_mate(1, 2)
+    gd.second_far(2)
+    gd.spot_to_mate(2, 2)
     gx.first_far()
     gx.second_send(2)
     gx.to_mate(0)
-    gd.second_far(0)
-    gd.second_far(R - 1)
-    gd.second_far(1)
-    gd.second_far(2)
-    gd.to_mate(2)
     gx.second_relay(0)
     cp_wd.wait()
     gd.mate_recv()
@@ -264,34 +285,49 @@
     gx.second_relay(1)
     cp_wg.wait()
     cp_wu.wait()
-    partial(0)
-    partial(1)
+    partial(0, 0)
+    partial(1, 0)
+    partial(2, 0)
+    partial(3, 0)
     scatter_first(0, 0)
-    partial(2)
     scatter_first(1, 0)
     gx.second_relay(2)
-    partial(3)
+    partial(0, 1)
     scatter_first(2, 0)
     scatter_first(3, 0)
+    pieces(scatter_raw, 0)
+    partial(1, 1)
+    partial(2, 1)
+    partial(3, 1)
     gx.to_mate(R - 1)
     gx.to_mate(1)
-    for g in range(1, GROUPS):
-        pieces(scatter_first, g)
+    pieces(scatter_first, 1)
+    partial(0, 2)
+    partial(1, 2)
+    partial(2, 2)
+    partial(3, 2)
     pieces(scatter_merge, 0)
-    transposes()
+    pieces(scatter_raw, 1)
+    pieces(scatter_first, 2)
     gx.second_far(0)
     gx.second_far(R - 1)
     gx.second_far(1)
     gx.second_far(2)
     gx.to_mate(2)
     pieces(scatter_merge, 1)
+    pieces(scatter_raw, 2)
+    transposes()
     pieces(scatter_second, 0)
+    pieces(scatter_merge, 2)
     pieces(scatter_second, 1)
     pieces(scatter_merge2, 0)
+    pieces(scatter_second, 2)
     pieces(scatter_merge2, 1)
     gx.mate_recv()
     pieces(scatter_last, 0)
+    pieces(scatter_merge2, 2)
     pieces(scatter_last, 1)
+    pieces(scatter_last, 2)
     for cp in sent:
         cp.wait_send()
     assert len(sent) == n_copies, len(sent)
@@ -317,7 +353,7 @@
         ffn = wd_loc.shape[0]
         tokens = tp * rows
         R = ring
-        n_copies = 2 * 2 * (4 + 4 * R + R) + 4 * GROUPS * 7
+        n_copies = 2 * 2 * (4 + 4 * R + R) - 2 + 2 * (R - 1) + 4 * len(GROUPS) * 7
         full = (R, R, CORES, rows, hidden)
         vm = pltpu.VMEM
         out_bytes = 2 * (rows * hidden + 2 * tokens * hidden + 3 * ffn * tokens)

time: 60.5 us -> 59.5 us (0.983)
  Pallas kernels: 59.4 us -> 58.4 us
    pallas_call x1, Pallas kernels: 10.2 us -> 9.5 us  [local_backward(): pl.pallas_call(weight_kernel, name='weight_grads', grid=(hidden // COL_TI...]
where the time goes in v3:
time: 59.5 us; the launch traced here: 59.1 us
  Pallas kernels  58.4 us (98%)
  between operations  0.64 us (1%)
    pallas_call x1, Pallas kernels, local_backward(): pl.pallas_call(lambda *refs: comm_kernel(R, n_copies, *refs), name='comm'...  48.9 us
    pallas_call x1, Pallas kernels, local_backward(): pl.pallas_call(weight_kernel, name='weight_grads', grid=(hidden // COL_TI...  9.5 us

profile of v3, /device:TPU:96, one launch (start us, length us, event | category | flops | bytes accessed | tf_op | source)
XLA Modules:
  0.0 59.1 jit_solution(15235766733189771805)
XLA Ops:
  0.6 48.9 %comm.1 = (bf16[8,5120]{1,0:T(8,128)(2,1)S(1)}, bf16[4,4,2,8,5120]{4,3,2,1,0:T(8,128)(2,1)S(1)}, bf16[4,4,2,8,5120]{4,3,2,1,0:T(8,128)(2,1)S(1)}, bf16[432,256]{...) custom-call(bf16[8,5120]{1,0:T(8,128)(2,1)} %refs_0_.1, bf16[8,5120]{1,0:T(8,128)(2,1)} %refs_1_.1, ...), custom_call_target="tpu_custom_call" | custom-call | tf_op jit(solution)/shard_map/comm/pallas_call | solution.py:360
  49.6 9.5 %weight_grads.1 = (f32[432,5120]{1,0:T(8,128)}, f32[432,5120]{1,0:T(8,128)}, f32[432,5120]{1,0:T(8,128)}, bf16[8,5120]{1,0:T(8,128)(2,1)}) custom-call(bf16[4,4,2,8,5120]{4,3,2,1,0:T(8,128)(2,1)S(1)} %get-tuple-element.14.xf, bf16[4,4,2,8,5120]{4,3,2,1,0:T(8,128)(2,1)S(1)} %get-tuple-element.15.dyf, bf16[432,256]{1,0:T(8,128)(2,1)S(1)} %get-tuple-element.16.dg_t, ...), custom_call_target="tpu_custom_call" | custom-call | tf_op jit(solution)/shard_map/weight_grads/pallas_call | solution.py:384
